TPU v7x, 32 devices: a whole 2x2x4 slice. The times are simulated.
32 devices in a mesh: grp: 1, sp: 32 (over z, y, x, core), ch: 1.
Axes of the slice: x: 2, y: 2, z: 4, core: 2. Of those that a mesh axis runs over, the one named last changes fastest.
Arguments:
- latents: bfloat16 [131072, 1024], P(('grp', 'sp')), may hold values from -6 to 6
- spectrum: bfloat16 [16, 64, 128, 1024], P(None, None, 'sp', 'ch'), may hold values from -4 to 4
- w_value: bfloat16 [1024, 1024], P('sp', 'ch'), may hold values from -0.1875 to 0.1875
- w_gate: bfloat16 [1024, 1024], P('sp', 'ch'), may hold values from -0.1875 to 0.1875
- w_out: bfloat16 [1024, 1024], P('sp'), may hold values from -0.1875 to 0.1875
- embed_table: bfloat16 [1024, 32768], P(('sp', 'ch')), may hold values from -12 to 12
- prompt_ids: int32 [256], P('grp'), may hold values from 0 to 32767
- noise_step: int32 [1], P('grp'), may hold values from 0 to 999
Outputs:
- denoised: bfloat16 [131072, 1024], P(('grp', 'sp', 'ch'))
All inputs are finite; a program needn't handle non-finite values.
Results may differ from a plain program's by a relative error of at most 0.013.
Values may be sent and summed in bfloat16 or wider, within the bound.
A program may use at most 128 MiB of HBM per device.

v0:
```python
import math

import jax
import jax.numpy as jnp
from jax import lax
from jax.sharding import PartitionSpec as P

TT = 16
HH = 64
WW = 128
C = 1024


def cas_table(length):
    position = jnp.arange(length, dtype=jnp.int32)
    product = position[:, None] * position[None, :] % length
    phase_angle = product.astype(jnp.float32) * (2.0 * math.pi / length)
    return ((jnp.cos(phase_angle) + jnp.sin(phase_angle)) / math.sqrt(length)).astype(jnp.bfloat16)


def step_embedding(noise_step, channel, channels):
    half_count = channels // 2
    lower_half = channel < half_count
    position = jnp.where(lower_half, channel, channel - half_count).astype(jnp.float32)
    frequency = jnp.exp(-math.log(10000.0) * position / half_count)
    phase_angle = noise_step[0].astype(jnp.float32) * frequency
    return jnp.where(lower_half, jnp.sin(phase_angle), jnp.cos(phase_angle))


def apply_table(form, table, operand):
    return jnp.einsum(form, table, operand, preferred_element_type=jnp.float32)


def local(latents, spectrum, w_value, w_gate, w_out, embed_table, prompt_ids, noise_step):
    row_count = latents.shape[0]
    chan_part = w_value.shape[1]
    full_value, full_gate, full_out = (
        lax.all_gather(w_value, "sp", axis=0, tiled=True),
        lax.all_gather(w_gate, "sp", axis=0, tiled=True),
        lax.all_gather(w_out, "sp", axis=0, tiled=True),
    )
    value_rows = jnp.dot(latents, full_value, preferred_element_type=jnp.float32).astype(
        jnp.bfloat16
    )
    gate_rows = jnp.dot(latents, full_gate, preferred_element_type=jnp.float32)
    cas_width = cas_table(WW)
    cas_height = cas_table(HH)
    cas_time = cas_table(TT)
    line_grid = value_rows.reshape(row_count // WW, WW, chan_part)
    width_spec = apply_table("kw,lwc->lkc", cas_width, line_grid).astype(jnp.bfloat16)
    pencil = lax.all_to_all(width_spec, "sp", split_axis=1, concat_axis=0, tiled=True)
    band_count = pencil.shape[1]
    pencil = pencil.reshape(TT, HH, band_count, chan_part)
    height_spec = apply_table("ah,thkc->takc", cas_height, pencil).astype(jnp.bfloat16)
    full_spec = apply_table("st,takc->sakc", cas_time, height_spec).astype(jnp.bfloat16)
    filtered = (full_spec.astype(jnp.float32) * spectrum.astype(jnp.float32)).astype(jnp.bfloat16)
    time_back = apply_table("ts,sakc->takc", cas_time, filtered).astype(jnp.bfloat16)
    height_back = apply_table("ha,takc->thkc", cas_height, time_back).astype(jnp.bfloat16)
    returned = lax.all_to_all(
        height_back.reshape(TT * HH, band_count, chan_part),
        "sp",
        split_axis=0,
        concat_axis=1,
        tiled=True,
    )
    mix_rows = apply_table("wk,lkc->lwc", cas_width, returned).reshape(row_count, chan_part)
    offset = lax.axis_index("ch") * chan_part
    local_pool = jnp.mean(jnp.take(embed_table, prompt_ids, axis=1).astype(jnp.float32), axis=1)
    pooled_all = lax.all_gather(local_pool, ("sp", "ch"), axis=0, tiled=True)
    pooled = lax.dynamic_slice_in_dim(pooled_all, offset, chan_part)
    channel = offset + jnp.arange(chan_part, dtype=jnp.int32)
    modulation = 1.0 + pooled + step_embedding(noise_step, channel, C)
    mixed_rows = (mix_rows * jax.nn.silu(gate_rows) * modulation[None, :]).astype(jnp.bfloat16)
    half_rows = row_count // lax.axis_size("ch")
    own_rows = lax.dynamic_slice_in_dim(full_out, offset, chan_part, 0)
    summed = lax.psum_scatter(
        jnp.dot(mixed_rows, own_rows, preferred_element_type=jnp.float32).astype(jnp.bfloat16),
        "ch",
        scatter_dimension=0,
        tiled=True,
    ).astype(jnp.float32)
    residual = lax.dynamic_slice_in_dim(latents, lax.axis_index("ch") * half_rows, half_rows, 0)
    return (residual.astype(jnp.float32) + summed).astype(jnp.bfloat16)


def solution(mesh):
    placed = (
        P(("grp", "sp"), None),
        P(None, None, "sp", "ch"),
        P("sp", "ch"),
        P("sp", "ch"),
        P("sp", None),
        P(("sp", "ch"), None),
        P("grp"),
        P("grp"),
    )
    return jax.shard_map(
        local, mesh=mesh, in_specs=placed, out_specs=P(("grp", "sp", "ch"), None), check_vma=False
    )
```

profile of v0, /device:TPU:0, one launch (start us, length us, event | category | flops | bytes accessed | tf_op | source)
XLA Modules:
  0.0 687.1 jit_solution(4367004813713135409)
XLA Ops:
  6.5 0.0 all-gather.4.cloned.1.call-start
  6.5 0.7 all-gather.4.cloned.1.call-update
  7.3 61.9 %all-gather.4.cloned.1.call-done = bf16[1024,1024]{1,0:T(8,128)(2,1)} async-done(((bf16[32,1024]{1,0:T(8,128)(2,1)}), bf16[1024,1024]{1,0:T(8,128)(2,1)}) %all-gather.4.cloned.1.call-update) | async-done | bytes 2097168 | tf_op jit(solution)/shard_map/all_gather | solution.py:38
  69.1 12.8 %convolution_convert_fusion = bf16[4096,1024]{1,0:T(8,128)(2,1)S(1)} fusion(bf16[4096,1024]{1,0:T(8,128)(2,1)} %param.8, bf16[1024,1024]{1,0:T(8,128)(2,1)} %all-gather.4.cloned.1.call-done), kind=kOutput, calls=%fused_computation.18 | convolution fusion | flops 8594128896 | bytes 18874368 | tf_op jit(solution)/shard_map/dot_general | solution.py:42
  82.0 5.1 convert_bitcast_fusion.2
  87.1 12.4 %copy.18 = bf16[32,128,1024]{2,0,1:T(8,128)(2,1)} copy(bf16[32,128,1024]{1,2,0:T(8,128)(2,1)} %convert_bitcast_fusion.2) | data formatting | bytes 16777216 | tf_op jit(solution)/shard_map/convert_element_type | solution.py:50
  99.5 187.2 %all_to_all.33 = bf16[32,128,1024]{2,0,1:T(8,128)(2,1)} all-to-all(bf16[32,128,1024]{2,0,1:T(8,128)(2,1)} %copy.18), channel_id=1, replica_groups=mesh['grp'=1,'sp'=32,'ch'=1] {'sp'}, dimensions={1} | all-to-all | bytes 16777216 | tf_op jit(solution)/shard_map/all_to_all | solution.py:51
  286.7 8.6 %copy.19 = bf16[32,32,4,1024]{3,1,0,2:T(8,128)(2,1)} copy(bf16[32,32,4,1024]{3,1,2,0:T(8,128)(2,1)} %bitcast.48) | data formatting | bytes 16777216 | tf_op jit(solution)/shard_map/all_to_all | solution.py:51
  295.3 9.1 %convert_bitcast_fusion.1 = bf16[16,64,4,1024]{3,1,2,0:T(8,128)(2,1)} fusion(bf16[16,64,4,1024]{3,1,0,2:T(8,128)(2,1)} %bitcast.49), kind=kOutput, calls=%fused_computation.16 | convolution fusion | flops 541134848 | bytes 16777216 | tf_op jit(solution)/shard_map/ah,thkc->takc/dot_general | solution.py:31
  304.4 26.9 %fusion.15 = bf16[16,64,4,1024]{3,0,2,1:T(8,128)(2,1)} fusion(bf16[16,64,4,1024]{3,2,1,0:T(4,128)(2,1)} %param.9, bf16[16,64,4,1024]{3,1,2,0:T(8,128)(2,1)} %convert_bitcast_fusion.1), kind=kOutput, calls=%fused_computation.19 | convolution fusion | flops 293609984 | bytes 25165824 | tf_op jit(solution)/shard_map/ts,sakc->takc/dot_general | solution.py:31
  331.3 17.6 %convert_bitcast_fusion = bf16[16,64,4,1024]{3,1,2,0:T(8,128)(2,1)} fusion(bf16[16,64,4,1024]{3,0,2,1:T(8,128)(2,1)} %fusion.15), kind=kOutput, calls=%fused_computation.14 | convolution fusion | flops 541134848 | bytes 16777216 | tf_op jit(solution)/shard_map/ha,takc->thkc/dot_general | solution.py:31
  348.9 8.6 %copy.24 = bf16[16,64,4,1024]{3,1,0,2:T(8,128)(2,1)} copy(bf16[16,64,4,1024]{3,1,2,0:T(8,128)(2,1)} %convert_bitcast_fusion) | data formatting | bytes 16777216 | tf_op jit(solution)/shard_map/convert_element_type | solution.py:58
  357.5 12.3 %copy.25 = bf16[1024,4,1024]{2,1,0:T(4,128)(2,1)} copy(bf16[1024,4,1024]{2,0,1:T(8,128)(2,1)} %bitcast.50) | data formatting | bytes 16777216 | tf_op jit(solution)/shard_map/reshape | solution.py:60
  369.8 0.0 copy-start
  369.8 3.8 all-to-all-start.1
  373.6 0.0 copy-start.1
  373.6 0.0 all-gather.6.cloned.1.call-start
  373.7 0.7 all-gather.6.cloned.1.call-update
  374.4 0.0 all-gather.8.cloned.1.call-start
  374.4 0.7 all-gather.8.cloned.1.call-update
  375.1 0.0 copy-done
  375.2 5.9 copy.28
  381.7 0.0 copy-done.1
  381.8 5.2 gather_fusion
  387.0 0.1 convert_reduce_fusion
  387.1 0.1 multiply_dynamic-update-slice_fusion
  387.2 210.4 %all-reduce = f32[1024]{0:T(1024)S(1)} all-reduce(f32[1024]{0:T(1024)S(1)} %multiply_dynamic-update-slice_fusion), channel_id=1, replica_groups=mesh['grp'=1,'sp'=32,'ch'=1] {'sp','ch'}, use_global_device_ids=true, to_apply=%add | all-reduce | flops 1024 | bytes 8192
  597.6 0.0 all-to-all-done.1
  597.6 9.6 %copy.26 = bf16[1024,4,1024]{2,0,1:T(8,128)(2,1)} copy(bf16[1024,4,1024]{2,1,0:T(4,128)(2,1)} %all-to-all-done.1) | data formatting | bytes 16777216 | tf_op jit(solution)/shard_map/all_to_all | solution.py:59
  607.3 12.2 %copy.27 = bf16[32,32,4,1024]{3,2,1,0:T(4,128)(2,1)} copy(bf16[32,32,4,1024]{3,0,1,2:T(8,128)(2,1)} %bitcast.51) | data formatting | bytes 16777216 | tf_op jit(solution)/shard_map/all_to_all | solution.py:59
  619.5 12.5 %all_to_all.30 = bf16[32,128,1024]{2,1,0:T(8,128)(2,1)} reshape(bf16[32,32,4,1024]{3,2,1,0:T(4,128)(2,1)} %copy.27) | data formatting | bytes 16777216 | tf_op jit(solution)/shard_map/all_to_all | solution.py:59
  631.9 11.7 %fusion.32 = f32[32,1024,128]{1,2,0:T(8,128)} fusion(bf16[32,128,1024]{2,1,0:T(8,128)(2,1)} %all_to_all.30), kind=kOutput, calls=%fused_computation.41 | convolution fusion | flops 1074020352 | bytes 25165824 | tf_op jit(solution)/shard_map/wk,lkc->lwc/dot_general | solution.py:31
  643.6 0.0 all-gather.6.cloned.1.call-done
  643.6 20.4 %fusion.1 = bf16[4096,1024]{1,0:T(8,128)(2,1)} fusion(f32[32,1024,128]{1,2,0:T(8,128)} %fusion.32, f32[1024]{0:T(1024)S(1)} %select_add_fusion, bf16[4096,1024]{1,0:T(8,128)(2,1)} %param.8, bf16[1024,1024]{1,0:T(8,128)(2,1)} %all-gather.6.cloned.1.call-done), kind=kOutput, calls=%fused_computation.3 | convolution fusion | flops 8619294720 | bytes 35655680 | tf_op jit(solution)/shard_map/dot_general | solution.py:45
  664.0 0.0 all-gather.8.cloned.1.call-done
  664.0 16.1 %add_convert_fusion = bf16[4096,1024]{1,0:T(8,128)(2,1)} fusion(bf16[4096,1024]{1,0:T(8,128)(2,1)} %param.8, bf16[4096,1024]{1,0:T(8,128)(2,1)} %fusion.1, bf16[1024,1024]{1,0:T(8,128)(2,1)} %all-gather.8.cloned.1.call-done), kind=kOutput, calls=%fused_computation.4 | convolution fusion | flops 8610906112 | bytes 27262976 | tf_op jit(solution)/shard_map/dot_general | solution.py:77
  (5 shorter events, 0.1 us)
Async XLA Ops:
  6.5 62.6 %all-gather.4.cloned.1.call-start = ((), (), s32[]{:S(2)}) async-start(), calls=%async_computation.2 | async-start | bytes 2162688 | tf_op jit(solution)/shard_map/all_gather | solution.py:38
  369.8 5.3 copy-start
  369.8 227.8 %all-to-all-start.1 = ((bf16[1024,4,1024]{2,1,0:T(4,128)(2,1)}), bf16[1024,4,1024]{2,1,0:T(4,128)(2,1)}, u32[]{:S(2)}, u32[]{:S(2)}) async-start(bf16[1024,4,1024]{2,1,0:T(4,128)(2,1)} %copy.25), calls=%async_computation.1 | async-start | bytes 16777216 | tf_op jit(solution)/shard_map/all_to_all | solution.py:59
  373.6 8.1 %copy-start.1 = (s32[256]{0:T(256)S(1)}, s32[256]{0:T(256)}, u32[]{:S(2)}) copy-start(s32[256]{0:T(256)} %param.14) | copy-start | bytes 3076
  373.6 270.0 %all-gather.6.cloned.1.call-start = ((), (), s32[]{:S(2)}) async-start(), calls=%async_computation.3 | async-start | bytes 2162688 | tf_op jit(solution)/shard_map/all_gather | solution.py:39
  374.4 289.6 %all-gather.8.cloned.1.call-start = ((), (), s32[]{:S(2)}) async-start(), calls=%async_computation.4 | async-start | bytes 2162688 | tf_op jit(solution)/shard_map/all_gather | solution.py:40
Sparse Core Ops, SparseCore 0:
  10.2 58.9 all-gather.3
  377.3 96.9 all-gather.5
  477.2 78.9 all-gather.7
where the time goes:
time: 695 us; the launch traced here: 687 us
  blocking collectives  398 us (57%)
  matrix products  120 us (17%)
  local copies, waits for them, and re-layouts  87.4 us (13%)
  waiting for transfers between devices  64 us (9%)
  between operations  14.3 us (2%)
    unnamed x1, blocking collectives  210 us
    all_to_all x1, blocking collectives, local(): lax.all_to_all(width_spec, 'sp', split_axis=1, concat_axis=0, tiled=True)  187 us
    dot_general x5, matrix products, apply_table(): return jnp.einsum(form, table, operand, preferred_element_type=jnp.float32)  70.4 us
    all_gather x1, waiting for transfers between devices, local(): lax.all_gather(w_value, 'sp', axis=0, tiled=True)  61.9 us
    all_to_all x3, local copies, waits for them, and re-layouts, local(): lax.all_to_all(height_back.reshape(TT * HH, band_count, chan_part), 'sp',...  34.3 us
    dot_general x1, matrix products, local(): gate_rows = jnp.dot(latents, full_gate, preferred_element_type=jnp.float32)  20.4 us
    dot_general x1, matrix products, local(): jnp.dot(mixed_rows, own_rows, preferred_element_type=jnp.float32)  16.1 us
  transfers between devices with their start and end apart: 4, of which 1 were waited for; matrix products, arithmetic and copies ran while one was open for 10% of the time, Pallas kernels for 0%

commit v1 on v0

v1 whole, which is shorter than its diff:
```python
import math

import jax
import jax.numpy as jnp
from jax import lax
from jax.experimental import pallas as pl
from jax.experimental.pallas import tpu as pltpu
from jax.sharding import PartitionSpec as P

TT = 16
HH = 64
WW = 128
C = 1024

TILE = 16


def cas_table(length):
    position = jnp.arange(length, dtype=jnp.int32)
    product = position[:, None] * position[None, :] % length
    phase_angle = product.astype(jnp.float32) * (2.0 * math.pi / length)
    return ((jnp.cos(phase_angle) + jnp.sin(phase_angle)) / math.sqrt(length)).astype(jnp.bfloat16)


def step_embedding(noise_step, channel, channels):
    half_count = channels // 2
    lower_half = channel < half_count
    position = jnp.where(lower_half, channel, channel - half_count).astype(jnp.float32)
    frequency = jnp.exp(-math.log(10000.0) * position / half_count)
    phase_angle = noise_step[0].astype(jnp.float32) * frequency
    return jnp.where(lower_half, jnp.sin(phase_angle), jnp.cos(phase_angle))


def widened(table, copies):
    length = table.shape[0]
    inner = jnp.eye(copies, dtype=table.dtype)
    both = table[:, None, :, None] * inner[None, :, None, :]
    return both.reshape(length * copies, length * copies)


def dot(left, right):
    return jnp.dot(left, right, preferred_element_type=jnp.float32)


def width_kernel(table_ref, latents_ref, out_ref):
    owners, rows, channels = out_ref.shape
    moved = dot(table_ref[...], latents_ref[...])
    out_ref[...] = moved.reshape(owners, rows, channels).astype(out_ref.dtype)


def width_forward(table, latents, owners, lines, band, group):
    channels = latents.shape[1]
    rows = group * WW
    cells = lines * WW
    return pl.pallas_call(
        width_kernel,
        grid=(lines // group,),
        in_specs=[
            pl.BlockSpec(table.shape, lambda g: (0, 0)),
            pl.BlockSpec((rows, channels), lambda g: (g, 0)),
        ],
        out_specs=pl.BlockSpec((owners, group * band, channels), lambda g: (0, g, 0)),
        out_shape=jax.ShapeDtypeStruct((owners, lines * band, channels), jnp.bfloat16),
        compiler_params=pltpu.CompilerParams(vmem_limit_bytes=48 * 2**20),
        cost_estimate=pl.CostEstimate(
            flops=2 * cells * table.shape[0] * channels,
            bytes_accessed=4 * cells * channels,
            transcendentals=0,
        ),
        name="width_forward",
    )(table, latents)


def plane_kernel(band, height_ref, time_ref, planes_ref, weight_ref, spectrum_ref, out_ref, spec):
    per_frame = HH * band
    width = out_ref.shape[1]
    pieces = per_frame // TILE
    weight = weight_ref[...].reshape(planes_ref.shape[1], width)

    def forward(t, carry):
        rows = pl.ds(pl.multiple_of(t * per_frame, per_frame), per_frame)
        value = dot(planes_ref[rows, :], weight).astype(jnp.bfloat16)
        spec[t] = dot(height_ref[...], value).astype(jnp.bfloat16)
        return carry

    lax.fori_loop(0, TT, forward, 0, unroll=4)

    def across(p, carry):
        rows = pl.ds(pl.multiple_of(p * TILE, TILE), TILE)
        block = spec[:, rows, :].reshape(TT * TILE, width)
        full = dot(time_ref[...], block)
        gain = spectrum_ref[:, rows, :].reshape(TT * TILE, width).astype(jnp.float32)
        filtered = (full * gain).astype(jnp.bfloat16)
        back = dot(time_ref[...], filtered).astype(jnp.bfloat16)
        spec[:, rows, :] = back.reshape(TT, TILE, width)
        return carry

    lax.fori_loop(0, pieces, across, 0, unroll=4)

    def backward(t, carry):
        rows = pl.ds(pl.multiple_of(t * per_frame, per_frame), per_frame)
        out_ref[rows, :] = dot(height_ref[...], spec[t]).astype(jnp.bfloat16)
        return carry

    lax.fori_loop(0, TT, backward, 0, unroll=4)


def plane_filter(height, time, planes, weight, spectrum, band):
    cells, channels = planes.shape
    shards, depth, chan_part = weight.shape
    width = min(256, chan_part)
    per_frame = HH * band
    return pl.pallas_call(
        lambda *refs: plane_kernel(band, *refs),
        grid=(chan_part // width,),
        in_specs=[
            pl.BlockSpec(height.shape, lambda g: (0, 0)),
            pl.BlockSpec(time.shape, lambda g: (0, 0)),
            pl.BlockSpec((cells, channels), lambda g: (0, 0)),
            pl.BlockSpec((shards, depth, width), lambda g: (0, 0, g)),
            pl.BlockSpec((TT, per_frame, width), lambda g: (0, 0, g)),
        ],
        out_specs=pl.BlockSpec((cells, width), lambda g: (0, g)),
        out_shape=jax.ShapeDtypeStruct((cells, chan_part), jnp.bfloat16),
        scratch_shapes=[pltpu.VMEM((TT, per_frame, width), jnp.bfloat16)],
        cost_estimate=pl.CostEstimate(
            flops=2 * cells * chan_part * (channels + 1024),
            bytes_accessed=2 * cells * (channels + 2 * chan_part),
            transcendentals=0,
        ),
        compiler_params=pltpu.CompilerParams(vmem_limit_bytes=56 * 2**20),
        name="plane_filter",
    )(height, time, planes, weight, spectrum)


def gate_kernel(latents_ref, gate_ref, scale_ref, out_ref):
    gate = dot(latents_ref[...], gate_ref[...].reshape(latents_ref.shape[1], out_ref.shape[1]))
    gate = gate / (1.0 + jnp.exp(-gate))
    out_ref[...] = (gate * scale_ref[...]).astype(out_ref.dtype)


def gate_rows(latents, gate_w, scale):
    cells, channels = latents.shape
    chan_part = gate_w.shape[2]
    rows = min(512, cells)
    return pl.pallas_call(
        gate_kernel,
        grid=(cells // rows,),
        in_specs=[
            pl.BlockSpec((rows, channels), lambda g: (g, 0)),
            pl.BlockSpec(gate_w.shape, lambda g: (0, 0, 0)),
            pl.BlockSpec((1, chan_part), lambda g: (0, 0)),
        ],
        out_specs=pl.BlockSpec((rows, chan_part), lambda g: (g, 0)),
        out_shape=jax.ShapeDtypeStruct((cells, chan_part), jnp.bfloat16),
        compiler_params=pltpu.CompilerParams(vmem_limit_bytes=48 * 2**20),
        cost_estimate=pl.CostEstimate(
            flops=2 * cells * channels * chan_part,
            bytes_accessed=2 * cells * (channels + chan_part),
            transcendentals=cells * chan_part,
        ),
        name="gate_rows",
    )(latents, gate_w, scale)


def mix_kernel(parts, residual, *refs):
    tables, backs = refs[:parts], refs[parts : 2 * parts]
    latents_ref, gate_ref, out_w_ref, out_ref = refs[2 * parts :]
    owners, rows, chan_part = backs[0].shape
    mix = dot(tables[0][...], backs[0][...].reshape(owners * rows, chan_part))
    for table_ref, back_ref in zip(tables[1:], backs[1:]):
        mix += dot(table_ref[...], back_ref[...].reshape(owners * rows, chan_part))
    mixed = (mix * gate_ref[...].astype(jnp.float32)).astype(jnp.bfloat16)
    projected = dot(mixed, out_w_ref[...].reshape(chan_part, out_ref.shape[1]))
    if residual:
        projected = latents_ref[...].astype(jnp.float32) + projected
    out_ref[...] = projected.astype(out_ref.dtype)


def mix_and_project(tables, backs, latents, gate, out_w, out_depth, group, residual):
    parts = len(backs)
    owners, rows_all, chan_part = backs[0].shape
    cells, channels = latents.shape
    groups = cells // (group * WW)
    rows = rows_all // groups
    cell_block = lambda wide: pl.BlockSpec((group * WW, wide), lambda g: (g, 0))
    return pl.pallas_call(
        lambda *refs: mix_kernel(parts, residual, *refs),
        grid=(groups,),
        in_specs=[
            *[pl.BlockSpec(table.shape, lambda g: (0, 0)) for table in tables],
            *[pl.BlockSpec((owners, rows, chan_part), lambda g: (0, g, 0)) for _ in backs],
            cell_block(channels),
            cell_block(chan_part),
            pl.BlockSpec((out_w.shape[0], out_depth, channels), lambda g: (0, 0, 0)),
        ],
        out_specs=cell_block(channels),
        out_shape=jax.ShapeDtypeStruct((cells, channels), jnp.bfloat16),
        compiler_params=pltpu.CompilerParams(vmem_limit_bytes=56 * 2**20),
        name="mix_and_project",
    )(*tables, *backs, latents, gate, out_w)


def exchange(blocks):
    return lax.all_to_all(blocks, "sp", split_axis=0, concat_axis=0, tiled=True)


def local(latents, spectrum, w_value, w_gate, w_out, embed_table, prompt_ids, noise_step):
    row_count, channels = latents.shape
    chan_part = w_value.shape[1]
    owners = lax.axis_size("sp")
    splits = lax.axis_size("ch")
    lines = row_count // WW
    band = WW // owners
    group = min(lines, max(1, TILE // band))

    parts = 2 if band % 2 == 0 else 1
    sub = band // parts

    table = cas_table(WW).reshape(owners, parts, 1, sub, 1, WW)
    same_line = jnp.eye(group, dtype=jnp.bfloat16).reshape(1, group, 1, group, 1)
    width_tables = [
        (table[:, part] * same_line).reshape(owners * group * sub, group * WW)
        for part in range(parts)
    ]
    height_table = widened(cas_table(HH), sub)
    time_table = widened(cas_table(TT), TILE)
    gains = spectrum.reshape(TT, HH, parts, sub, chan_part)

    full_value = lax.all_gather(w_value, "sp", axis=0)

    full_gate = lax.all_gather(w_gate, "sp", axis=0)
    local_pool = jnp.mean(jnp.take(embed_table, prompt_ids, axis=1).astype(jnp.float32), axis=1)
    offset = lax.axis_index("ch") * chan_part
    depth = w_out.shape[0]
    if splits == 1:
        first = local_pool.astype(jnp.bfloat16)
        rest = local_pool - first.astype(jnp.float32)
        second = rest.astype(jnp.bfloat16)
        third = (rest - second.astype(jnp.float32)).astype(jnp.bfloat16)
        terms = jnp.stack([first, second, third])
        terms = jnp.pad(terms, ((0, TILE - 3), (0, channels - terms.shape[1])))
        full_out = lax.all_gather(jnp.concatenate([w_out, terms], axis=0), "sp", axis=0)
    else:
        pooled_all = lax.all_gather(local_pool, ("sp", "ch"), axis=0, tiled=True)
        pooled = lax.dynamic_slice_in_dim(pooled_all, offset, chan_part)
        rows_out = lax.all_gather(w_out, "sp", axis=0, tiled=True)
        full_out = lax.dynamic_slice_in_dim(rows_out, offset, chan_part, 0)[None]
        depth = chan_part

    planes, backs = [], []
    for part in range(parts):
        sent = width_forward(width_tables[part], latents, owners, lines, sub, group)
        if planes:
            sent, planes[-1], full_value = lax.optimization_barrier((sent, planes[-1], full_value))
        planes.append(exchange(sent))
    for part in range(parts):
        filtered = plane_filter(
            height_table,
            time_table,
            planes[part].reshape(TT * HH * sub, channels),
            full_value,
            gains[:, :, part].reshape(TT, HH * sub, chan_part),
            sub,
        ).reshape(owners, lines * sub, chan_part)
        if backs:
            filtered, backs[-1], full_gate = lax.optimization_barrier(
                (filtered, backs[-1], full_gate)
            )
        elif parts > 1:
            filtered, planes[-1], full_out = lax.optimization_barrier(
                (filtered, planes[-1], full_out)
            )
        backs.append(exchange(filtered))

    if splits == 1:
        pooled = full_out[:, depth : depth + 3, : local_pool.shape[0]].astype(jnp.float32)
        pooled = jnp.sum(pooled, axis=1).reshape(chan_part)
    channel = offset + jnp.arange(chan_part, dtype=jnp.int32)
    modulation = 1.0 + pooled + step_embedding(noise_step, channel, C)

    gate = gate_rows(latents, full_gate, modulation[None, :])
    mixed = mix_and_project(
        [width_table.T for width_table in width_tables],
        backs,
        latents,
        gate,
        full_out,
        depth,
        group,
        splits == 1,
    )
    if splits == 1:
        return mixed
    half_rows = row_count // splits
    summed = lax.psum_scatter(mixed, "ch", scatter_dimension=0, tiled=True).astype(jnp.float32)
    residual = lax.dynamic_slice_in_dim(latents, lax.axis_index("ch") * half_rows, half_rows, 0)
    return (residual.astype(jnp.float32) + summed).astype(jnp.bfloat16)


def solution(mesh):
    placed = (
        P(("grp", "sp"), None),
        P(None, None, "sp", "ch"),
        P("sp", "ch"),
        P("sp", "ch"),
        P("sp", None),
        P(("sp", "ch"), None),
        P("grp"),
        P("grp"),
    )
    return jax.shard_map(
        local, mesh=mesh, in_specs=placed, out_specs=P(("grp", "sp", "ch"), None), check_vma=False
    )
```

time: 695 us -> 474 us (0.68)
  blocking collectives: 398 us -> 0 us
  waiting for transfers between devices: 64 us -> 245 us
  Pallas kernels: 0 us -> 127 us
  matrix products: 120 us -> 0 us
  local copies, waits for them, and re-layouts: 87.4 us -> 62.6 us
  starting transfers between devices: 3.9 us -> 19.8 us
    unnamed x1 -> x0, blocking collectives: 210 us -> none
    all_to_all x1 -> x0, blocking collectives: 187 us -> none  [local(): lax.all_to_all(width_spec, 'sp', split_axis=1, concat_axis=0, tiled=True)]
    pallas_call x0 -> x6, Pallas kernels: none -> 127 us  [the longest x2 77.9 us: plane_filter(): pl.pallas_call(lambda *refs: plane_kernel(band, *refs), grid=(chan_part /...]
    all_to_all x1 -> x4, waiting for transfers between devices: 0.01 us -> 122 us  [exchange(): return lax.all_to_all(blocks, 'sp', split_axis=0, concat_axis=0, tiled=True)]
    dot_general x8 -> x0, matrix products: 120 us -> none  [the longest x5 70.4 us: apply_table(): return jnp.einsum(form, table, operand, preferred_element_type=jnp.float32)]
    all_gather x3, waiting for transfers between devices: 61.9 us -> 122 us  [the longest x1 78.1 us: local(): full_value = lax.all_gather(w_value, 'sp', axis=0)]
    all_to_all x4 -> x0, local copies, waits for them, and re-layouts: 42.9 us -> none  [the longest x3 34.3 us: local(): lax.all_to_all(height_back.reshape(TT * HH, band_count, chan_part), 'sp',...]
    convert_element_type x2 -> x0, local copies, waits for them, and re-layouts: 21 us -> none  [the longest x1 12.4 us: local(): apply_table('kw,lwc->lkc', cas_width, line_grid).astype(jnp.bfloat16)]
  transfers between devices with their start and end apart: 4 -> 7, of which waited for: 1 -> 7; matrix products, arithmetic and copies ran while one was open for 10% -> 13% of each run, Pallas kernels for 0% -> 21%
where the time goes in v1:
time: 474 us; the launch traced here: 472 us
  waiting for transfers between devices  245 us (52%)
  Pallas kernels  127 us (27%)
  local copies, waits for them, and re-layouts  62.6 us (13%)
  starting transfers between devices  19.8 us (4%)
  between operations  14 us (3%)
    all_to_all x4, waiting for transfers between devices, exchange(): return lax.all_to_all(blocks, 'sp', split_axis=0, concat_axis=0, tiled=True)  122 us
    all_gather x1, waiting for transfers between devices, local(): full_value = lax.all_gather(w_value, 'sp', axis=0)  78.1 us
    pallas_call x2, Pallas kernels, plane_filter(): pl.pallas_call(lambda *refs: plane_kernel(band, *refs), grid=(chan_part /...  77.9 us
    all_gather x1, waiting for transfers between devices, local(): full_gate = lax.all_gather(w_gate, 'sp', axis=0)  41.5 us
    pallas_call x1, Pallas kernels, mix_and_project(): pl.pallas_call(lambda *refs: mix_kernel(parts, residual, *refs), grid=(gr...  19.8 us
    all_to_all x4, starting transfers between devices, exchange(): return lax.all_to_all(blocks, 'sp', split_axis=0, concat_axis=0, tiled=True)  19.5 us
    unnamed x16, local copies, waits for them, and re-layouts  18.4 us
    reshape x1, local copies, waits for them, and re-layouts, local(): gains = spectrum.reshape(TT, HH, parts, sub, chan_part)  17.5 us
  transfers between devices with their start and end apart: 7, of which 7 were waited for; matrix products, arithmetic and copies ran while one was open for 13% of the time, Pallas kernels for 21%

profile of v1, /device:TPU:0, one launch (start us, length us, event | category | flops | bytes accessed | tf_op | source)
XLA Modules:
  0.0 472.2 jit_solution(7177597898888992940)
XLA Ops:
  6.5 0.3 multiply_convert_fusion
  7.0 0.3 broadcast_multiply_fusion.2
  7.3 7.5 %width_forward.3 = bf16[32,64,1024]{2,1,0:T(8,128)(2,1)S(1)} custom-call(bf16[256,512]{1,0:T(8,128)(2,1)S(1)} %bitcast.45, bf16[4096,1024]{1,0:T(8,128)(2,1)} %refs_4_.1), custom_call_target="tpu_custom_call" | custom-call | flops 2147483648 | bytes 16777216 | tf_op jit(solution)/shard_map/width_forward/pallas_call | solution.py:55
  14.8 0.0 copy-start.1
  14.8 2.0 copy-done.1
  16.8 7.5 %all-to-all-start = ((bf16[32,64,1024]{2,1,0:T(8,128)(2,1)}), bf16[32,64,1024]{2,1,0:T(8,128)(2,1)}, u32[]{:S(2)}, u32[]{:S(2)}) async-start(bf16[32,64,1024]{2,1,0:T(8,128)(2,1)} %copy-done.1), calls=%async_computation | async-start | bytes 8388608 | tf_op jit(solution)/shard_map/all_to_all | solution.py:205
  24.2 0.0 all-gather.7.cloned.1.call-start
  24.3 0.7 all-gather.7.cloned.1.call-update
  25.0 7.5 %width_forward.2 = bf16[32,64,1024]{2,1,0:T(8,128)(2,1)S(1)} custom-call(bf16[256,512]{1,0:T(8,128)(2,1)S(1)} %bitcast.47, bf16[4096,1024]{1,0:T(8,128)(2,1)} %refs_4_.1), custom_call_target="tpu_custom_call" | custom-call | flops 2147483648 | bytes 16777216 | tf_op jit(solution)/shard_map/width_forward/pallas_call | solution.py:55
  32.5 2.0 copy-done
  34.5 78.1 %all-gather.7.cloned.1.call-done = bf16[1024,1024]{1,0:T(8,128)(2,1)} async-done(((bf16[32,1024]{1,0:T(8,128)(2,1)}), bf16[1024,1024]{1,0:T(8,128)(2,1)}) %all-gather.7.cloned.1.call-update) | async-done | bytes 2097168 | tf_op jit(solution)/shard_map/all_gather | solution.py:230
  112.6 15.4 %all-to-all-done = bf16[32,64,1024]{2,1,0:T(8,128)(2,1)} async-done(((bf16[32,64,1024]{2,1,0:T(8,128)(2,1)}), bf16[32,64,1024]{2,1,0:T(8,128)(2,1)}, u32[]{:S(2)}, u32[]{:S(2)}) %all-to-all-start) | async-done | bytes 4194336 | tf_op jit(solution)/shard_map/all_to_all | solution.py:205
  128.0 3.9 all-to-all-start.1
  131.9 0.0 copy-start.5
  131.9 0.0 all-gather.9.cloned.1.call-start
  132.0 5.9 %copy.24 = bf16[32,32768]{0,1:T(8,128)(2,1)} copy(bf16[32,32768]{1,0:T(8,128)(2,1)S(1)} %copy-done.3) | data formatting | bytes 4194304 | tf_op args[5]
  137.9 5.2 %gather_fusion = bf16[256,32]{1,0:T(8,128)(2,1)S(1)} fusion(bf16[32,32768]{0,1:T(8,128)(2,1)} %copy.24, s32[1024]{0:T(1024)S(1)} %pad_clamp_fusion), kind=kCustom, calls=%fused_computation | custom fusion | bytes 33792 | tf_op jit(solution)/shard_map/jit(_take)/gather | solution.py:233
  143.1 0.1 convert_reduce_fusion
  143.3 0.6 pad_maximum_fusion
  143.9 0.0 all-gather.9.cloned.1.call-update
  143.9 17.5 %reshape.298 = bf16[16,64,2,2,1024]{4,3,2,1,0:T(2,128)(2,1)} reshape(bf16[16,64,4,1024]{3,2,1,0:T(4,128)(2,1)} %param.9) | data formatting | bytes 16777216 | tf_op jit(solution)/shard_map/reshape | solution.py:228
  161.4 8.4 %slice_bitcast_fusion = (bf16[16,64,1,2,1024]{4,3,1,0,2:T(2,128)(2,1)}, bf16[16,64,1,2,1024]{4,3,1,0,2:T(2,128)(2,1)}) fusion(bf16[16,64,2,2,1024]{4,3,2,1,0:T(2,128)(2,1)} %reshape.298), kind=kLoop, calls=%fused_computation.1 | loop fusion | bytes 16777216
  169.8 7.2 %reshape_squeeze.6.refs_4_ = bf16[16,128,1024]{2,1,0:T(8,128)(2,1)} reshape(bf16[16,64,1,2,1024]{4,3,1,0,2:T(2,128)(2,1)} %get-tuple-element.24) | data formatting | bytes 8388608 | tf_op jit(solution)/shard_map/reshape;squeeze | solution.py:263
  177.0 0.2 multiply_convert_fusion.1
  177.2 0.7 broadcast_multiply_fusion
  177.9 3.8 mul.316.refs_0_
  181.7 0.1 multiply_convert_fusion.2
  181.7 0.1 broadcast_multiply_fusion.1
  181.9 1.6 mul.325.refs_1_
  183.5 38.9 %plane_filter.2 = bf16[2048,1024]{1,0:T(8,128)(2,1)} custom-call(bf16[128,128]{1,0:T(8,128)(2,1)} %mul.316.refs_0_, bf16[256,256]{1,0:T(8,128)(2,1)} %mul.325.refs_1_, bf16[2048,1024]{1,0:T(8,128)(2,1)} %bitcast.5.refs_2_, bf16[32,32,1024]{2,1,0:T(8,128)(2,1)} %bitcast.58, bf16[16,128,1024]{2,1,0:T(8,128)(2,1)} %reshape_squeeze.6.refs_4_), custom_call_target="tpu_custom_call" | custom-call | flops 8589934592 | bytes 12582912 | tf_op jit(solution)/shard_map/plane_filter/pallas_call | solution.py:113
  222.4 2.4 all-gather.9.cloned.1.call-done
  224.8 15.5 %all-to-all-done.1 = bf16[32,64,1024]{2,1,0:T(8,128)(2,1)} async-done(((bf16[32,64,1024]{2,1,0:T(8,128)(2,1)}), bf16[32,64,1024]{2,1,0:T(8,128)(2,1)}, u32[]{:S(2)}, u32[]{:S(2)}) %all-to-all-start.1) | async-done | bytes 4194336 | tf_op jit(solution)/shard_map/all_to_all | solution.py:205
  240.3 4.3 all-to-all-start.2
  244.6 0.2 all-gather.11.cloned.1.call-start
  244.8 0.5 all-gather.11.cloned.1.call-update
  245.3 7.2 %reshape_squeeze.7.refs_4_ = bf16[16,128,1024]{2,1,0:T(8,128)(2,1)} reshape(bf16[16,64,1,2,1024]{4,3,1,0,2:T(2,128)(2,1)} %get-tuple-element.23) | data formatting | bytes 8388608 | tf_op jit(solution)/shard_map/reshape;squeeze | solution.py:263
  252.5 39.0 %plane_filter.3 = bf16[2048,1024]{1,0:T(8,128)(2,1)} custom-call(bf16[128,128]{1,0:T(8,128)(2,1)} %mul.316.refs_0_, bf16[256,256]{1,0:T(8,128)(2,1)} %mul.325.refs_1_, bf16[2048,1024]{1,0:T(8,128)(2,1)} %bitcast.9.refs_2_, bf16[32,32,1024]{2,1,0:T(8,128)(2,1)} %bitcast.59, bf16[16,128,1024]{2,1,0:T(8,128)(2,1)} %reshape_squeeze.7.refs_4_), custom_call_target="tpu_custom_call" | custom-call | flops 8589934592 | bytes 12582912 | tf_op jit(solution)/shard_map/plane_filter/pallas_call | solution.py:113
  291.5 41.5 %all-gather.11.cloned.1.call-done = bf16[1024,1024]{1,0:T(8,128)(2,1)} async-done(((bf16[32,1024]{1,0:T(8,128)(2,1)}), bf16[1024,1024]{1,0:T(8,128)(2,1)}) %all-gather.11.cloned.1.call-update) | async-done | bytes 2097168 | tf_op jit(solution)/shard_map/all_gather | solution.py:232
  333.0 15.4 %all-to-all-done.2.refs_2_ = bf16[32,64,1024]{2,1,0:T(8,128)(2,1)} async-done(((bf16[32,64,1024]{2,1,0:T(8,128)(2,1)}), bf16[32,64,1024]{2,1,0:T(8,128)(2,1)}, u32[]{:S(2)}, u32[]{:S(2)}) %all-to-all-start.2) | async-done | bytes 4194336 | tf_op jit(solution)/shard_map/all_to_all | solution.py:205
  348.3 3.9 all-to-all-start.3
  352.2 0.8 copy.20
  353.0 0.8 copy.22
  354.5 0.9 convert_reduce_fusion.1
  355.4 0.1 add.143
  355.5 0.1 fusion.32.scale_ref
  355.7 14.7 %gate_rows.1.refs_5_ = bf16[4096,1024]{1,0:T(8,128)(2,1)} custom-call(bf16[4096,1024]{1,0:T(8,128)(2,1)} %refs_4_.1, bf16[32,32,1024]{2,1,0:T(8,128)(2,1)S(1)} %bitcast.49, f32[1,1024]{1,0:T(1,128)S(1)} %fusion.32.scale_ref), custom_call_target="tpu_custom_call" | custom-call | flops 8589934592 | bytes 16777216 | tf_op jit(solution)/shard_map/gate_rows/pallas_call | solution.py:146
  370.4 75.5 %all-to-all-done.3.refs_3_ = bf16[32,64,1024]{2,1,0:T(8,128)(2,1)} async-done(((bf16[32,64,1024]{2,1,0:T(8,128)(2,1)}), bf16[32,64,1024]{2,1,0:T(8,128)(2,1)}, u32[]{:S(2)}, u32[]{:S(2)}) %all-to-all-start.3) | async-done | bytes 4194336 | tf_op jit(solution)/shard_map/all_to_all | solution.py:205
  445.9 19.8 %mix_and_project.1 = bf16[4096,1024]{1,0:T(8,128)(2,1)} custom-call(bf16[512,256]{1,0:T(8,128)(2,1)} %bitcast.54, bf16[512,256]{1,0:T(8,128)(2,1)} %bitcast.55, bf16[32,64,1024]{2,1,0:T(8,128)(2,1)} %all-to-all-done.2.refs_2_, bf16[32,64,1024]{2,1,0:T(8,128)(2,1)} %all-to-all-done.3.refs_3_, bf16[4096,1024]{1,0:T(8,128)(2,1)} %refs_4_.1, ...), custom_call_target="tpu_custom_call" | custom-call | tf_op jit(solution)/shard_map/mix_and_project/pallas_call | solution.py:187
  (24 shorter events, 0.2 us)
Async XLA Ops:
  14.8 2.0 copy-start.1
  16.8 111.2 %all-to-all-start = ((bf16[32,64,1024]{2,1,0:T(8,128)(2,1)}), bf16[32,64,1024]{2,1,0:T(8,128)(2,1)}, u32[]{:S(2)}, u32[]{:S(2)}) async-start(bf16[32,64,1024]{2,1,0:T(8,128)(2,1)} %copy-done.1), calls=%async_computation | async-start | bytes 8388608 | tf_op jit(solution)/shard_map/all_to_all | solution.py:205
  24.2 88.4 %all-gather.7.cloned.1.call-start = ((), (), s32[]{:S(2)}) async-start(), calls=%async_computation.4 | async-start | bytes 2162688 | tf_op jit(solution)/shard_map/all_gather | solution.py:230
  32.5 2.0 copy-start
  128.0 4.0 copy-start.3
  128.0 112.3 %all-to-all-start.1 = ((bf16[32,64,1024]{2,1,0:T(8,128)(2,1)}), bf16[32,64,1024]{2,1,0:T(8,128)(2,1)}, u32[]{:S(2)}, u32[]{:S(2)}) async-start(bf16[32,64,1024]{2,1,0:T(8,128)(2,1)} %copy-done), calls=%async_computation.1 | async-start | bytes 8388608 | tf_op jit(solution)/shard_map/all_to_all | solution.py:205
  131.9 6.0 %copy-start.5 = (s32[256]{0:T(256)S(1)}, s32[256]{0:T(256)}, u32[]{:S(2)}) copy-start(s32[256]{0:T(256)} %param.14) | copy-start | bytes 3076
  131.9 11.4 %copy-start.4 = (bf16[32,1024]{1,0:T(8,128)(2,1)S(1)}, bf16[32,1024]{1,0:T(8,128)(2,1)}, u32[]{:S(2)}) copy-start(bf16[32,1024]{1,0:T(8,128)(2,1)} %param.12) | copy-start | bytes 196612
  131.9 92.9 %all-gather.9.cloned.1.call-start = ((), (), s32[]{:S(2)}) async-start(), calls=%async_computation.5 | async-start | bytes 3244032 | tf_op jit(solution)/shard_map/all_gather | solution.py:243
  240.3 108.0 %all-to-all-start.2 = ((bf16[32,64,1024]{2,1,0:T(8,128)(2,1)}), bf16[32,64,1024]{2,1,0:T(8,128)(2,1)}, u32[]{:S(2)}, u32[]{:S(2)}) async-start(bf16[32,64,1024]{2,1,0:T(8,128)(2,1)} %bitcast.50), calls=%async_computation.2 | async-start | bytes 8388608 | tf_op jit(solution)/shard_map/all_to_all | solution.py:205
  244.6 88.4 %all-gather.11.cloned.1.call-start = ((), (), s32[]{:S(2)}) async-start(), calls=%async_computation.6 | async-start | bytes 2162688 | tf_op jit(solution)/shard_map/all_gather | solution.py:232
  348.3 7.3 %copy-start.2 = (bf16[1024,1024]{1,0:T(8,128)(2,1)S(1)}, bf16[1024,1024]{1,0:T(8,128)(2,1)}, u32[]{:S(2)}) copy-start(bf16[1024,1024]{1,0:T(8,128)(2,1)} %all-gather.11.cloned.1.call-done) | copy-start | bytes 6291460
  348.3 97.6 %all-to-all-start.3 = ((bf16[32,64,1024]{2,1,0:T(8,128)(2,1)}), bf16[32,64,1024]{2,1,0:T(8,128)(2,1)}, u32[]{:S(2)}, u32[]{:S(2)}) async-start(bf16[32,64,1024]{2,1,0:T(8,128)(2,1)} %bitcast.51), calls=%async_computation.3 | async-start | bytes 8388608 | tf_op jit(solution)/shard_map/all_to_all | solution.py:205
Sparse Core Ops, SparseCore 0:
  27.9 84.6 all-gather.6
  144.1 80.7 all-gather.8
  248.2 84.6 all-gather.10
